TPU v7x, 32 devices: a whole 2x2x4 slice. The times are simulated.
32 devices in a mesh: expert: 4 (over y, x), dp: 2 (over core), mp: 4 (over z).
Axes of the slice: x: 2, y: 2, z: 4, core: 2. Of those that a mesh axis runs over, the one named last changes fastest.
Arguments:
- tokens: bfloat16 [96, 4096], P(('expert', 'dp'), 'mp'), may hold values from -6 to 6
- routes: int32 [96, 2], P(('expert', 'dp')), may hold values from 0 to 3, all different within a row; in each aligned block of 12 rows (0 to 11, 12 to 23, ...) at most 9 rows name the same one
- router_weight: bfloat16 [4096, 4], P('mp'), may hold values from -0.09375 to 0.09375
- gate_weight: bfloat16 [4, 4096, 16384], P('expert', None, ('dp', 'mp')), may hold values from -0.09375 to 0.09375
- up_weight: bfloat16 [4, 4096, 16384], P('expert', None, ('dp', 'mp')), may hold values from -0.09375 to 0.09375
- down_weight: bfloat16 [4, 16384, 4096], P('expert', ('dp', 'mp')), may hold values from -0.0625 to 0.0625
Outputs:
- mixed: bfloat16 [96, 4096], P(('expert', 'dp'), 'mp')
Inputs may be any that keep to these rules, and one draw needn't show every extreme that they name: `routes`: each row names two different experts; among the 12 rows of one device (aligned blocks) no expert is named more than 9 times, a bound that some block reaches.
All inputs are finite; a program needn't handle non-finite values.
Results may differ from a plain program's by a relative error of at most 0.0049.
Values may be sent and summed in bfloat16 or wider, within the bound.
No kernel may reach another device: no remote copies, remote signals or barrier semaphores. Data moves between devices by JAX's collectives and lax.ppermute only.
A program may use at most 128 MiB of HBM per device.

v0:
```python
import jax
import jax.numpy as jnp
from jax import lax
from jax.sharding import PartitionSpec as P


def per_device(tokens, routes, router_weight, gate_weight, up_weight, down_weight):
    row_count = tokens.shape[0]
    experts = lax.axis_size("expert")
    capacity = max(2, (6 * row_count + 2 * experts - 1) // (2 * experts))
    partial_logits = jnp.dot(tokens, router_weight, preferred_element_type=jnp.float32)
    logits = lax.psum(partial_logits, "mp")
    labels = jnp.arange(experts, dtype=jnp.int32)
    onehot = (routes[:, :, None] == labels).astype(jnp.int32)
    chosen = jnp.sum(onehot.astype(jnp.float32) * logits[:, None, :], axis=2)
    weights = jnp.stack(
        [jax.nn.sigmoid(chosen[:, 0] - chosen[:, 1]), jax.nn.sigmoid(chosen[:, 1] - chosen[:, 0])],
        axis=1,
    )
    flat_hot = onehot.reshape(row_count * 2, experts)
    before = jnp.cumsum(flat_hot, axis=0) - flat_hot
    position = jnp.sum(flat_hot * before, axis=1)
    places = (position[:, None] == jnp.arange(capacity, dtype=jnp.int32)).astype(jnp.float32)
    assign = (flat_hot.astype(jnp.float32)[:, :, None] * places[:, None, :]).reshape(
        row_count, 2, experts, capacity
    )
    select = jnp.sum(assign, axis=1).astype(jnp.bfloat16)
    combine = jnp.sum(assign * weights[:, :, None, None], axis=1).reshape(
        row_count, experts * capacity
    )
    full_rows = lax.all_gather(tokens, "mp", axis=1, tiled=True)
    full_width = full_rows.shape[1]
    buffer = jnp.einsum(
        "tec,td->ecd", select, full_rows, preferred_element_type=jnp.float32
    ).astype(jnp.bfloat16)
    arrived = lax.all_to_all(buffer, "expert", split_axis=0, concat_axis=0, tiled=True)
    inputs = lax.all_gather(
        arrived.reshape(experts * capacity, full_width), "dp", axis=0, tiled=True
    )
    gate_part = jnp.dot(inputs, gate_weight[0], preferred_element_type=jnp.float32)
    up_part = jnp.dot(inputs, up_weight[0], preferred_element_type=jnp.float32)
    hidden = (jax.nn.silu(gate_part) * up_part).astype(jnp.bfloat16)
    summed = lax.psum_scatter(
        jnp.dot(hidden, down_weight[0], preferred_element_type=jnp.float32),
        "dp",
        scatter_dimension=0,
        tiled=True,
    )
    returned = lax.all_to_all(
        summed.reshape(experts, capacity, full_width),
        "expert",
        split_axis=0,
        concat_axis=0,
        tiled=True,
    )
    partial_mix = jnp.dot(
        combine,
        returned.reshape(experts * capacity, full_width),
        precision=lax.Precision.HIGHEST,
        preferred_element_type=jnp.float32,
    )
    mixed_out = lax.psum_scatter(partial_mix, "mp", scatter_dimension=1, tiled=True)
    return mixed_out.astype(jnp.bfloat16)


def solution(mesh):
    return jax.shard_map(
        per_device,
        mesh=mesh,
        in_specs=(
            P(("expert", "dp"), "mp"),
            P(("expert", "dp"), None),
            P("mp", None),
            P("expert", None, ("dp", "mp")),
            P("expert", None, ("dp", "mp")),
            P("expert", ("dp", "mp"), None),
        ),
        out_specs=P(("expert", "dp"), "mp"),
        check_vma=False,
    )
```

profile of v0, /device:TPU:0, one launch (start us, length us, event | category | flops | bytes accessed | tf_op | source)
XLA Modules:
  0.0 128.2 jit_solution(11685603426469671855)
XLA Ops:
  6.5 0.8 copy.17
  7.3 0.7 convert_convert_fusion
  8.0 0.1 eq.48
  8.1 0.1 fusion.21
  8.2 0.2 select_reduce_fusion
  8.4 0.1 eq.52
  8.5 0.1 copy.18
  8.6 15.3 %all_gather.6 = bf16[12,4096]{1,0:T(8,128)(2,1)S(1)} all-gather(bf16[12,1024]{1,0:T(8,128)(2,1)} %param.6), channel_id=1, replica_groups=mesh['expert'=4,'dp'=2,'mp'=4] {'mp'}, dimensions={1}, use_global_device_ids=true | all-gather | bytes 122880 | tf_op jit(solution)/shard_map/all_gather | solution.py:31
  23.9 0.0 copy-done
  23.9 0.9 fusion.23
  24.8 12.0 %psum.7 = f32[12,4]{0,1:T(4,128)S(1)} all-reduce(f32[12,4]{0,1:T(4,128)S(1)} %fusion.23), channel_id=1, replica_groups=mesh['expert'=4,'dp'=2,'mp'=4] {'mp'}, use_global_device_ids=true, to_apply=%region_2.0 | all-reduce | flops 48 | bytes 384 | tf_op jit(solution)/shard_map/psum | solution.py:12
  36.8 0.7 multiply_reduce_fusion.1
  37.6 0.3 convolution_convert_fusion
  37.8 10.6 %all_to_all.10 = bf16[4,9,4096]{2,1,0:T(8,128)(2,1)S(1)} all-to-all(bf16[4,9,4096]{2,1,0:T(8,128)(2,1)S(1)} %convolution_convert_fusion), channel_id=1, replica_groups=mesh['expert'=4,'dp'=2,'mp'=4] {'expert'}, dimensions={0} | all-to-all | bytes 589824 | tf_op jit(solution)/shard_map/all_to_all | solution.py:36
  48.5 0.1 reshape.62
  48.6 2.3 %all-gather = bf16[2,36,4096]{2,1,0:T(8,128)(2,1)S(1)} all-gather(bf16[1,36,4096]{2,1,0:T(8,128)(2,1)S(1)} %reshape.62), channel_id=1, replica_groups=mesh['expert'=4,'dp'=2,'mp'=4] {'dp'}, dimensions={0}, use_global_device_ids=true | all-gather | bytes 884736 | tf_op jit(solution)/shard_map/all_gather | solution.py:37
  50.9 0.1 reshape.63
  51.0 8.8 %fusion.5 = f32[72,2048]{1,0:T(8,128)S(1)} fusion(bf16[72,4096]{1,0:T(8,128)(2,1)S(1)} %reshape.63, bf16[1,4096,2048]{2,1,0:T(8,128)(2,1)} %param.9), kind=kOutput, calls=%fused_computation.4 | convolution fusion | flops 1207959552 | bytes 17956864 | tf_op jit(solution)/shard_map/dot_general | solution.py:40
  59.8 0.0 copy-start.1
  59.9 16.6 %fusion.1 = f32[72,4096]{1,0:T(8,128)S(1)} fusion(bf16[1,2048,4096]{2,1,0:T(8,128)(2,1)} %param.11, bf16[72,4096]{1,0:T(8,128)(2,1)S(1)} %reshape.63, bf16[1,4096,2048]{2,1,0:T(8,128)(2,1)} %param.10, f32[72,2048]{1,0:T(8,128)S(1)} %fusion.5), kind=kOutput, calls=%fused_computation | convolution fusion | flops 2416803840 | bytes 35913728 | tf_op jit(solution)/shard_map/dot_general | solution.py:44
  76.4 4.1 %fusion = f32[40,4096]{1,0:T(8,128)S(1)} fusion(f32[72,4096]{1,0:T(8,128)S(1)} %fusion.1), kind=kCustom, calls=%all-reduce-scatter | all-reduce-scatter fusion | flops 327681 | bytes 1835520
  80.6 2.3 %collective-permute-start = (f32[4,4096]{1,0:T(4,128)S(1)}, f32[4,4096]{1,0:T(4,128)S(1)}, u32[]{:S(2)}, u32[]{:S(2)}) collective-permute-start(f32[4,4096]{1,0:T(4,128)S(1)} %slice.10), channel_id=1, source_target_pairs={{0,4},{1,5},{2,6},{3,7},{8,12},{9,13},{10,14},{11,15},{16,20},{17,... | collective-permute-start | bytes 196616
  82.9 0.6 dynamic-slice.4
  84.1 0.0 collective-permute-done
  84.2 0.4 concatenate
  84.6 0.1 constant_dynamic-slice_fusion
  84.6 0.1 reshape.61
  84.7 17.0 %all_to_all.11 = f32[4,9,4096]{2,1,0:T(8,128)S(1)} all-to-all(f32[4,9,4096]{2,1,0:T(8,128)S(1)} %reshape.61), channel_id=1, replica_groups=mesh['expert'=4,'dp'=2,'mp'=4] {'expert'}, dimensions={0} | all-to-all | bytes 1179648 | tf_op jit(solution)/shard_map/all_to_all | solution.py:49
  101.7 1.3 %convolution_bitcast_fusion = f32[12,4096]{1,0:T(8,128)} fusion(f32[4,9,4096]{2,1,0:T(8,128)S(1)} %all_to_all.11, f32[12,4,9]{0,1,2:T(4,128)S(1)} %get-tuple-element.5), kind=kOutput, calls=%fused_computation.7 | convolution fusion | flops 21233664 | bytes 788160 | tf_op jit(solution)/shard_map/dot_general | solution.py:56
  103.0 0.0 reduce-scatter.4.cloned.1.call-update
  103.1 16.8 %reduce-scatter.4.cloned.1.call-done = f32[12,1024]{1,0:T(8,128)} async-done(((f32[12,4096]{1,0:T(8,128)}), f32[12,1024]{1,0:T(8,128)}) %reduce-scatter.4.cloned.1.call-update) | async-done | bytes 49168 | tf_op jit(solution)/shard_map/reduce_scatter | solution.py:62
  119.9 1.5 %convert_element_type.44 = bf16[12,1024]{1,0:T(8,128)(2,1)} convert(f32[12,1024]{1,0:T(8,128)} %reduce-scatter.4.cloned.1.call-done) | non-fusion elementwise | flops 12288 | bytes 73728 | tf_op jit(solution)/shard_map/convert_element_type | solution.py:63
  (9 shorter events, 0.1 us)
Async XLA Ops:
  6.5 17.3 %copy-start = (bf16[1024,4]{0,1:T(4,128)(2,1)S(1)}, bf16[1024,4]{0,1:T(4,128)(2,1)}, u32[]{:S(2)}) copy-start(bf16[1024,4]{0,1:T(4,128)(2,1)} %param.8) | copy-start | bytes 24580
  6.5 113.4 %reduce-scatter.4.cloned.1.call-start = ((), (), s32[]{:S(2)}) async-start(), calls=%async_computation.3 | async-start | bytes 327680 | tf_op jit(solution)/shard_map/reduce_scatter | solution.py:62
  59.8 23.1 %copy-start.1 = (u32[32]{0:T(128)S(1)}, u32[32]{0:T(128)}, u32[]{:S(2)}) copy-start(u32[32]{0:T(128)} %constant.19) | copy-start | bytes 388
  80.6 3.5 %collective-permute-start = (f32[4,4096]{1,0:T(4,128)S(1)}, f32[4,4096]{1,0:T(4,128)S(1)}, u32[]{:S(2)}, u32[]{:S(2)}) collective-permute-start(f32[4,4096]{1,0:T(4,128)S(1)} %slice.10), channel_id=1, source_target_pairs={{0,4},{1,5},{2,6},{3,7},{8,12},{9,13},{10,14},{11,15},{16,20},{17,... | collective-permute-start | bytes 196616
Sparse Core Ops, SparseCore 0:
  103.2 16.6 reduce-scatter.3
where the time goes:
time: 129 us; the launch traced here: 128 us
  blocking collectives  61.4 us (48%)
  matrix products  27.9 us (22%)
  waiting for transfers between devices  16.9 us (13%)
  between operations  14.2 us (11%)
  other arithmetic  3.21 us (2%)
  local copies, waits for them, and re-layouts  2.45 us (2%)
  starting transfers between devices  2.28 us (2%)
    all_to_all x1, blocking collectives, per_device(): lax.all_to_all(summed.reshape(experts, capacity, full_width), 'expert', s...  17 us
    reduce_scatter x1, waiting for transfers between devices, per_device(): lax.psum_scatter(partial_mix, 'mp', scatter_dimension=1, tiled=True)  16.8 us
    dot_general x1, matrix products, per_device(): jnp.dot(hidden, down_weight[0], preferred_element_type=jnp.float32)  16.6 us
    all_gather x1, blocking collectives, per_device(): full_rows = lax.all_gather(tokens, 'mp', axis=1, tiled=True)  15.3 us
    psum x1, blocking collectives, per_device(): logits = lax.psum(partial_logits, 'mp')  12 us
    all_to_all x1, blocking collectives, per_device(): lax.all_to_all(buffer, 'expert', split_axis=0, concat_axis=0, tiled=True)  10.6 us
    dot_general x1, matrix products, per_device(): jnp.dot(inputs, gate_weight[0], preferred_element_type=jnp.float32)  8.83 us
    unnamed x1, blocking collectives  4.14 us
  transfers between devices with their start and end apart: 2, of which 1 were waited for; matrix products, arithmetic and copies ran while one was open for 0% of the time, Pallas kernels for 0%

commit v1 on v0

--- a/solution.py
+++ b/solution.py
@@ -9,7 +9,9 @@
     experts = lax.axis_size("expert")
     capacity = max(2, (6 * row_count + 2 * experts - 1) // (2 * experts))
     partial_logits = jnp.dot(tokens, router_weight, preferred_element_type=jnp.float32)
-    logits = lax.psum(partial_logits, "mp")
+    logits = partial_logits
+    for hop in (1, 2):
+        logits = logits + lax.ppermute(logits, "mp", [(dev, dev ^ hop) for dev in range(4)])
     labels = jnp.arange(experts, dtype=jnp.int32)
     onehot = (routes[:, :, None] == labels).astype(jnp.int32)
     chosen = jnp.sum(onehot.astype(jnp.float32) * logits[:, None, :], axis=2)

time: 129 us -> 122 us (0.946)
  blocking collectives: 61.4 us -> 47.7 us
  starting transfers between devices: 2.28 us -> 7.99 us
    psum x1 -> x0, blocking collectives: 12 us -> none  [per_device(): logits = lax.psum(partial_logits, 'mp')]
    ppermute x0 -> x2, starting transfers between devices: none -> 5.71 us  [per_device(): lax.ppermute(logits, 'mp', [(dev, dev ^ hop) for dev in range(4)])]
    all_gather x1, blocking collectives: 15.3 us -> 13.6 us  [per_device(): full_rows = lax.all_gather(tokens, 'mp', axis=1, tiled=True)]
  transfers between devices with their start and end apart: 2 -> 4, of which waited for: 1 -> 1; matrix products, arithmetic and copies ran while one was open for 0% -> 2% of each run, Pallas kernels for 0% -> 0%
where the time goes in v1:
time: 122 us
  blocking collectives  47.7 us (39%)
  matrix products  27.9 us (23%)
  waiting for transfers between devices  17.7 us (15%)
  between operations  14.2 us (12%)
  starting transfers between devices  7.99 us (7%)
  other arithmetic  3.24 us (3%)
  local copies, waits for them, and re-layouts  3.13 us (3%)
    reduce_scatter x1, waiting for transfers between devices, per_device(): lax.psum_scatter(partial_mix, 'mp', scatter_dimension=1, tiled=True)  17.7 us
    all_to_all x1, blocking collectives, per_device(): lax.all_to_all(summed.reshape(experts, capacity, full_width), 'expert', s...  17 us
    dot_general x1, matrix products, per_device(): jnp.dot(hidden, down_weight[0], preferred_element_type=jnp.float32)  16.6 us
    all_gather x1, blocking collectives, per_device(): full_rows = lax.all_gather(tokens, 'mp', axis=1, tiled=True)  13.6 us
    all_to_all x1, blocking collectives, per_device(): lax.all_to_all(buffer, 'expert', split_axis=0, concat_axis=0, tiled=True)  10.6 us
    dot_general x1, matrix products, per_device(): jnp.dot(inputs, gate_weight[0], preferred_element_type=jnp.float32)  8.83 us
    ppermute x2, starting transfers between devices, per_device(): lax.ppermute(logits, 'mp', [(dev, dev ^ hop) for dev in range(4)])  5.71 us
    unnamed x1, blocking collectives  4.14 us
  transfers between devices with their start and end apart: 4, of which 1 were waited for; matrix products, arithmetic and copies ran while one was open for 2% of the time, Pallas kernels for 0%

profile of v1, /device:TPU:0, one launch (start us, length us, event | category | flops | bytes accessed | tf_op | source)
XLA Modules:
  0.0 121.8 jit_solution(9032143782555172413)
XLA Ops:
  6.5 0.7 copy-done
  7.2 0.9 fusion.23
  8.1 3.1 %collective-permute-start = (f32[12,4]{0,1:T(4,128)S(1)}, f32[12,4]{0,1:T(4,128)S(1)}, u32[]{:S(2)}, u32[]{:S(2)}) collective-permute-start(f32[12,4]{0,1:T(4,128)S(1)} %fusion.23), channel_id=1, source_target_pairs={{0,1},{1,0},{2,3},{3,2},{4,5},{5,4},{6,7},{7,6},{8,9},{9,8},{10,11... | collective-permute-start | bytes 584 | tf_op jit(solution)/shard_map/ppermute | solution.py:14
  11.2 0.8 copy.17
  11.9 0.1 eq.48
  12.0 0.1 fusion.21
  12.1 0.2 select_reduce_fusion
  12.3 0.1 eq.52
  12.4 0.1 copy.18
  12.5 0.7 convert_convert_fusion
  13.2 2.7 %collective-permute-start.1 = (f32[12,4]{0,1:T(4,128)S(1)}, f32[12,4]{0,1:T(4,128)S(1)}, u32[]{:S(2)}, u32[]{:S(2)}) collective-permute-start(f32[12,4]{0,1:T(4,128)S(1)} %add.22), channel_id=1, source_target_pairs={{0,2},{1,3},{2,0},{3,1},{4,6},{5,7},{6,4},{7,5},{8,10},{9,11},{10,... | collective-permute-start | bytes 584 | tf_op jit(solution)/shard_map/ppermute | solution.py:14
  15.9 13.6 %all_gather.6 = bf16[12,4096]{1,0:T(8,128)(2,1)S(1)} all-gather(bf16[12,1024]{1,0:T(8,128)(2,1)} %param.6), channel_id=1, replica_groups=mesh['expert'=4,'dp'=2,'mp'=4] {'mp'}, dimensions={1}, use_global_device_ids=true | all-gather | bytes 122880 | tf_op jit(solution)/shard_map/all_gather | solution.py:33
  29.5 0.7 multiply_reduce_fusion.1
  30.3 0.3 convolution_convert_fusion
  30.6 10.6 %all_to_all.10 = bf16[4,9,4096]{2,1,0:T(8,128)(2,1)S(1)} all-to-all(bf16[4,9,4096]{2,1,0:T(8,128)(2,1)S(1)} %convolution_convert_fusion), channel_id=1, replica_groups=mesh['expert'=4,'dp'=2,'mp'=4] {'expert'}, dimensions={0} | all-to-all | bytes 589824 | tf_op jit(solution)/shard_map/all_to_all | solution.py:38
  41.2 0.1 reshape.62
  41.3 2.3 %all-gather = bf16[2,36,4096]{2,1,0:T(8,128)(2,1)S(1)} all-gather(bf16[1,36,4096]{2,1,0:T(8,128)(2,1)S(1)} %reshape.62), channel_id=1, replica_groups=mesh['expert'=4,'dp'=2,'mp'=4] {'dp'}, dimensions={0}, use_global_device_ids=true | all-gather | bytes 884736 | tf_op jit(solution)/shard_map/all_gather | solution.py:39
  43.6 0.1 reshape.63
  43.7 8.8 %fusion.5 = f32[72,2048]{1,0:T(8,128)S(1)} fusion(bf16[72,4096]{1,0:T(8,128)(2,1)S(1)} %reshape.63, bf16[1,4096,2048]{2,1,0:T(8,128)(2,1)} %param.9), kind=kOutput, calls=%fused_computation.4 | convolution fusion | flops 1207959552 | bytes 17956864 | tf_op jit(solution)/shard_map/dot_general | solution.py:42
  52.6 0.0 copy-start.1
  52.6 16.6 %fusion.1 = f32[72,4096]{1,0:T(8,128)S(1)} fusion(bf16[1,2048,4096]{2,1,0:T(8,128)(2,1)} %param.11, bf16[72,4096]{1,0:T(8,128)(2,1)S(1)} %reshape.63, bf16[1,4096,2048]{2,1,0:T(8,128)(2,1)} %param.10, f32[72,2048]{1,0:T(8,128)S(1)} %fusion.5), kind=kOutput, calls=%fused_computation | convolution fusion | flops 2416803840 | bytes 35913728 | tf_op jit(solution)/shard_map/dot_general | solution.py:46
  69.2 4.1 %fusion = f32[40,4096]{1,0:T(8,128)S(1)} fusion(f32[72,4096]{1,0:T(8,128)S(1)} %fusion.1), kind=kCustom, calls=%all-reduce-scatter | all-reduce-scatter fusion | flops 327681 | bytes 1835520
  73.3 2.3 %collective-permute-start.2 = (f32[4,4096]{1,0:T(4,128)S(1)}, f32[4,4096]{1,0:T(4,128)S(1)}, u32[]{:S(2)}, u32[]{:S(2)}) collective-permute-start(f32[4,4096]{1,0:T(4,128)S(1)} %slice.10), channel_id=1, source_target_pairs={{0,4},{1,5},{2,6},{3,7},{8,12},{9,13},{10,14},{11,15},{16,20},{17,... | collective-permute-start | bytes 196616
  75.6 0.6 dynamic-slice.4
  76.9 0.4 concatenate
  77.3 0.1 constant_dynamic-slice_fusion
  77.4 0.1 reshape.61
  77.5 17.0 %all_to_all.11 = f32[4,9,4096]{2,1,0:T(8,128)S(1)} all-to-all(f32[4,9,4096]{2,1,0:T(8,128)S(1)} %reshape.61), channel_id=1, replica_groups=mesh['expert'=4,'dp'=2,'mp'=4] {'expert'}, dimensions={0} | all-to-all | bytes 1179648 | tf_op jit(solution)/shard_map/all_to_all | solution.py:51
  94.5 1.3 %convolution_bitcast_fusion = f32[12,4096]{1,0:T(8,128)} fusion(f32[4,9,4096]{2,1,0:T(8,128)S(1)} %all_to_all.11, f32[12,4,9]{0,1,2:T(4,128)S(1)} %get-tuple-element.5), kind=kOutput, calls=%fused_computation.7 | convolution fusion | flops 21233664 | bytes 788160 | tf_op jit(solution)/shard_map/dot_general | solution.py:58
  95.8 0.0 reduce-scatter.4.cloned.1.call-update
  95.8 17.7 %reduce-scatter.4.cloned.1.call-done = f32[12,1024]{1,0:T(8,128)} async-done(((f32[12,4096]{1,0:T(8,128)}), f32[12,1024]{1,0:T(8,128)}) %reduce-scatter.4.cloned.1.call-update) | async-done | bytes 49168 | tf_op jit(solution)/shard_map/reduce_scatter | solution.py:64
  113.5 1.5 %convert_element_type.44 = bf16[12,1024]{1,0:T(8,128)(2,1)} convert(f32[12,1024]{1,0:T(8,128)} %reduce-scatter.4.cloned.1.call-done) | non-fusion elementwise | flops 12288 | bytes 73728 | tf_op jit(solution)/shard_map/convert_element_type | solution.py:65
  (14 shorter events, 0.2 us)
Async XLA Ops:
  6.5 0.7 copy-start
  6.5 107.0 %reduce-scatter.4.cloned.1.call-start = ((), (), s32[]{:S(2)}) async-start(), calls=%async_computation.3 | async-start | bytes 327680 | tf_op jit(solution)/shard_map/reduce_scatter | solution.py:64
  8.1 5.1 %collective-permute-start = (f32[12,4]{0,1:T(4,128)S(1)}, f32[12,4]{0,1:T(4,128)S(1)}, u32[]{:S(2)}, u32[]{:S(2)}) collective-permute-start(f32[12,4]{0,1:T(4,128)S(1)} %fusion.23), channel_id=1, source_target_pairs={{0,1},{1,0},{2,3},{3,2},{4,5},{5,4},{6,7},{7,6},{8,9},{9,8},{10,11... | collective-permute-start | bytes 584 | tf_op jit(solution)/shard_map/ppermute | solution.py:14
  13.2 16.3 %collective-permute-start.1 = (f32[12,4]{0,1:T(4,128)S(1)}, f32[12,4]{0,1:T(4,128)S(1)}, u32[]{:S(2)}, u32[]{:S(2)}) collective-permute-start(f32[12,4]{0,1:T(4,128)S(1)} %add.22), channel_id=1, source_target_pairs={{0,2},{1,3},{2,0},{3,1},{4,6},{5,7},{6,4},{7,5},{8,10},{9,11},{10,... | collective-permute-start | bytes 584 | tf_op jit(solution)/shard_map/ppermute | solution.py:14
  52.6 23.1 %copy-start.1 = (u32[32]{0:T(128)S(1)}, u32[32]{0:T(128)}, u32[]{:S(2)}) copy-start(u32[32]{0:T(128)} %constant.19) | copy-start | bytes 388
  73.3 3.5 %collective-permute-start.2 = (f32[4,4096]{1,0:T(4,128)S(1)}, f32[4,4096]{1,0:T(4,128)S(1)}, u32[]{:S(2)}, u32[]{:S(2)}) collective-permute-start(f32[4,4096]{1,0:T(4,128)S(1)} %slice.10), channel_id=1, source_target_pairs={{0,4},{1,5},{2,6},{3,7},{8,12},{9,13},{10,14},{11,15},{16,20},{17,... | collective-permute-start | bytes 196616
Sparse Core Ops, SparseCore 0:
  95.9 17.5 reduce-scatter.3
